TPU v7x, 512 devices: a whole 4x4x16 slice. The times are simulated.
512 devices in a mesh: ctx: 128 (over z, x, y_hi), head: 4 (over y_lo, core).
Axes of the slice: x: 4, y: 4 (y_hi: 2, y_lo: 2; y = y_hi * 2 + y_lo), z: 16, core: 2. Of those that a mesh axis runs over, the one named last changes fastest.
Arguments:
- queries: bfloat16 [8192, 8192], P('ctx', 'head'), may hold values from -6 to 6
- keys: bfloat16 [8192, 128], P('ctx'), may hold values from -6 to 6
- key_gain: float32 [128], replicated, may hold values from 0.25 to 1.75
- key_bias: float32 [128], replicated, may hold values from -0.5 to 0.5
- head_weights: bfloat16 [8192, 64], P('ctx', 'head'), may hold values from -6 to 6
- positions: int32 [8192], P('ctx'), may hold values from 0 to 6143, as said below
Outputs:
- index_scores: float32 [8192, 8192], P(('ctx', 'head'))
Inputs may be any that keep to these rules, and one draw needn't show every extreme that they name: `positions`: positions of packed documents: the first 6144 tokens form one document and the rest is split into one to three documents at drawn points; a token's position counts from its document's first token.
All inputs are finite; a program needn't handle non-finite values.
Results may differ from a plain program's by a relative error of at most 0.0095.
Values may be sent and summed in bfloat16 or wider, within the bound.
No kernel may reach another device: no remote copies, remote signals or barrier semaphores. Data moves between devices by JAX's collectives and lax.ppermute only.
A program may use at most 64 MiB of HBM per device.

v0:
```python
import functools
import math

import jax
import jax.numpy as jnp
import numpy as np
from jax import lax
from jax.experimental import pallas as pl
from jax.experimental.pallas import tpu as pltpu
from jax.sharding import Mesh
from jax.sharding import PartitionSpec as P

H = 64
DH = 128
ROPE = 64
ROWS = 64
SUB = 16
HG = 16
QT = HG * ROWS
PEERS = 8
SLOTS = 3
NK = PEERS * ROWS
PLANE = 512
GROUP = 4 * PLANE
LAST_EARLY = 3
SCALE = 1.0 / math.sqrt(H * DH)


def yarn_frequencies(rope_dims):
    half_dims = rope_dims // 2
    exponent = np.arange(0, rope_dims, 2) / rope_dims
    extra_freq = 1.0 / 10000.0**exponent
    inter_freq = extra_freq / 40.0

    def correction(beta):
        return rope_dims * math.log(4096.0 / (beta * 2.0 * math.pi)) / (2.0 * math.log(10000.0))

    low_dim = max(math.floor(correction(32.0)), 0)
    high_dim = min(math.ceil(correction(1.0)), rope_dims - 1)
    ramp_values = np.clip((np.arange(half_dims) - low_dim) / (high_dim - low_dim), 0.0, 1.0)
    return (inter_freq * ramp_values + extra_freq * (1.0 - ramp_values)).astype(np.float32)


def turned(raw, gain, bias, cosine, sine):
    v = raw.astype(jnp.float32)
    c = v - jnp.mean(v, axis=-1, keepdims=True)
    s = jnp.mean(c * c, axis=-1, keepdims=True)
    k = c * lax.rsqrt(s + 1e-06) * gain + bias
    return rotated(jnp.concatenate([k, k], 0).T, cosine, sine).T[:ROWS].astype(jnp.bfloat16)


def rotated(x, cosine, sine):
    half = ROPE // 2
    cosine = jnp.concatenate([cosine, cosine], 1)
    sine = jnp.concatenate([sine, sine], 1)
    a, b = x[:half], x[half:ROPE]
    return jnp.concatenate([a * cosine - b * sine, b * cosine + a * sine, x[ROPE:]], 0)


def column(row, n, shift):
    m = row.shape[1]
    at = lax.broadcasted_iota(jnp.int32, (n, m), 0) + shift
    lane = lax.broadcasted_iota(jnp.int32, (n, m), 1)
    return jnp.sum(jnp.where(at == lane, jnp.broadcast_to(row, (n, m)), 0.0), axis=1, keepdims=True)


def where_am_i():
    z_hi, z_lo = lax.axis_index("zh"), lax.axis_index("zl")
    ctx = ((z_hi * 4 + z_lo) * 4 + lax.axis_index("x")) * 2 + lax.axis_index("yh")
    head = lax.axis_index("yl") * 2 + lax.axis_index("core")
    return head, ctx * ROWS, z_hi, z_lo ^ head ^ (2 * lax.axis_index("yh"))


def turn_queries(q, w, cosine, sine, out):
    wf = w[...].astype(jnp.float32)
    both = jnp.concatenate([wf[: HG // 2], wf[HG // 2 :]], 1)
    for p in range(HG // 2):
        x = jnp.concatenate(
            [q[:, h * DH : (h + 1) * DH].astype(jnp.float32) for h in (p, p + HG // 2)], 0
        ).T
        at = slice(p * DH, (p + 1) * DH)
        out[:DH, at] = rotated(x, cosine, sine).astype(jnp.bfloat16)
        out[DH:, at] = jnp.broadcast_to(both[p : p + 1], (16, DH)).astype(jnp.bfloat16)


def turn(k):
    plane = lax.axis_index("zh") * 4 + lax.axis_index("zl")
    group_2 = lax.axis_index("zh") == 2
    return (plane <= LAST_EARLY, (plane > LAST_EARLY) & jnp.logical_not(group_2), group_2)[k]


def fetch(pairs, sems):
    copies = [pltpu.make_async_copy(src, dst, sems.at[i]) for i, (src, dst) in enumerate(pairs)]
    for c in copies:
        c.start()
    for c in copies:
        c.wait()


def prepare_kernel(k, *refs):
    n = 7
    far, refs = refs[:n], refs[n:]
    if k:
        before, refs = refs[0], refs[2:]
    out_q, out_k, held, sems = refs[0], refs[1], refs[2 : 2 + n], refs[2 + n]

    if k:
        @pl.when(jnp.logical_not(turn(k)))
        def _():
            out_k[...] = before[...]

    @pl.when(turn(k))
    def _():
        fetch(zip(far, held), sems)
        keys, gain, bias, pos, freq, w, q = held
        angle = freq[...] * pos[...].astype(jnp.float32)
        cosine, sine = jnp.cos(angle), jnp.sin(angle)
        out_k[...] = turned(keys[...], gain[...], bias[...], cosine, sine)
        turn_queries(q, w, cosine, sine, out_q)


def prepare(k, sources, before=()):
    n = len(sources)
    return pl.pallas_call(
        functools.partial(prepare_kernel, k),
        out_shape=(pltpu.VMEM((DH + 16, QT), jnp.bfloat16), pltpu.VMEM((ROWS, DH), jnp.bfloat16)),
        in_specs=[ANY] * n + [VMEM] * len(before),
        out_specs=(VMEM, VMEM),
        input_output_aliases={n + 1: 0} if k else {},
        scratch_shapes=[pltpu.VMEM(x.shape, x.dtype) for x in sources] + [pltpu.SemaphoreType.DMA((n,))],
    )(*sources, *[near(x) for x in before])


def pack_kernel(own_0, own_13, own_2, from_0, near_by, far_off, out):
    group = lax.axis_index("zh")
    own = jnp.where(group == 0, own_0[...], jnp.where(group == 2, own_2[...], own_13[...]))
    last = jnp.where(group == 1, from_0[...], near_by[...])
    for slot, x in enumerate((own, last, far_off[...])):
        for d in range(PEERS):
            out[d, slot] = x


def score_kernel(q0, q1, q2, q3, k, pos, out):
    _, first, group, z = where_am_i()
    row = lax.broadcasted_iota(jnp.int32, (ROWS, 1), 0) + first
    doc = row - column(pos[...].astype(jnp.float32), ROWS, 0).astype(jnp.int32)

    def one(slot, start, n):
        peers = slice(start // ROWS, (start + n) // ROWS)
        kk = k[peers, slot].reshape(n, DH)
        acc = jnp.zeros((n, DH), jnp.float32)
        for q in (q0, q1, q2, q3):
            w = q[DH : DH + 1, :].astype(jnp.float32)
            for c in range(0, QT, 512):
                s = jnp.dot(kk, q[:DH, c : c + 512], preferred_element_type=jnp.float32)
                for p in range(0, 512, DH):
                    acc = acc + jnp.maximum(s[:, p : p + DH], 0.0) * w[:, c + p : c + p + DH]
        acc = acc.T
        acc = acc[:ROWS] + acc[ROWS:]
        key = plane_start(slot) + start + lax.broadcasted_iota(jnp.int32, (1, n), 1)
        seen = (key >= doc) & (key <= row)
        out[:, slot, :, start : start + n] = (
            jnp.where(seen, acc * SCALE, 0.0).astype(jnp.bfloat16).reshape(4, SUB, n)
        )

    def plane_start(slot):
        return (group - slot) * GROUP + z * PLANE

    for start, n in ((0, 128), (128, 128), (256, 256)):
        reached = plane_start(0) + start < first + ROWS

        @pl.when(reached)
        def _():
            one(0, start, n)

        @pl.when(jnp.logical_not(reached))
        def _():
            out[:, 0, :, start : start + n] = jnp.zeros((4, SUB, n), jnp.bfloat16)

    for slot in range(1, SLOTS):
        live = (slot <= group) & (group < 3)

        @pl.when(live)
        def _():
            one(slot, 0, NK)

        @pl.when(jnp.logical_not(live))
        def _():
            out[:, slot] = jnp.zeros((4, SUB, NK), jnp.bfloat16)


def place_kernel(parts, out):
    head, _, group, z = where_am_i()
    out[...] = jnp.zeros_like(out)
    live = jnp.where(group == 3, 1, group + 1)
    for slot in range(SLOTS):
        @pl.when(slot < live)
        def _():
            for j in range(4):
                at = pl.multiple_of((group - slot) * GROUP + (z ^ head ^ j) * PLANE, PLANE)
                out[:, pl.ds(at, PLANE)] = parts[j, slot].astype(jnp.float32)


VMEM = pl.BlockSpec(memory_space=pltpu.VMEM)
ANY = pl.BlockSpec(memory_space=pl.ANY)


def call(kernel, shape, dtype, *args, inside=True):
    if inside:
        out = pltpu.VMEM(shape, dtype)
    else:
        out = jax.ShapeDtypeStruct(shape, dtype)
    return pl.pallas_call(kernel, out_shape=out, in_specs=[VMEM] * len(args), out_specs=VMEM)(*args)


def near(x):
    return pltpu.with_memory_space_constraint(x, pltpu.VMEM)


LINE = ("zh", "zl", "yh", "yl", "core")


def hop(src, dst, cross):
    def at(g, z, j):
        return (g * 4 + z) * 8 + j

    return [
        (at(src, z, j), at(dst, z ^ m if cross else z, j))
        for z in range(4) for j in range(8) for m in ((j & 3) ^ (j >> 2) * 2,)
    ]


NEAR = [[(x * 2 + h) * 2 + (t ^ h) for x in range(4) for h in range(2)] for t in range(2)]


def program(queries, keys, key_gain, key_bias, head_weights, positions):
    freq = jnp.asarray(yarn_frequencies(ROPE)[:, None])
    gain, bias = key_gain.reshape(1, DH), key_bias.reshape(1, DH)
    pos = positions.reshape(1, ROWS)
    weights = head_weights.T

    sources = (keys, gain, bias, pos, freq, weights, queries)

    q, mine = prepare(0, sources)
    own_0 = lax.ppermute(mine, LINE, hop(0, 0, True))
    from_0 = lax.ppermute(own_0, LINE, hop(0, 1, False))
    q, mine = prepare(1, sources, (mine, q))
    own_13 = lax.ppermute(mine, LINE, hop(1, 1, True) + hop(3, 3, True))
    far_off = lax.ppermute(from_0, LINE, hop(1, 2, False))
    q0, mine = prepare(2, sources, (mine, q))
    swap = [(0, 1), (1, 0)]
    q1 = lax.ppermute(q0, "yl", swap)
    near_by = lax.ppermute(own_13, LINE, hop(1, 2, False))
    own_2 = lax.ppermute(mine, LINE, hop(2, 2, True))
    q2 = lax.ppermute(q0, "core", swap)
    q3 = lax.ppermute(q1, "core", swap)

    sent = call(
        pack_kernel, (PEERS, SLOTS, ROWS, DH), jnp.bfloat16,
        near(own_0), near(own_13), near(own_2), near(from_0), near(near_by), near(far_off),
    )
    k_all = lax.all_to_all(
        sent, ("x", "yh", "yl"), 0, 0, axis_index_groups=NEAR, tiled=True
    )

    parts = call(
        score_kernel, (4, SLOTS, SUB, NK), jnp.bfloat16,
        near(q0), near(q1), near(q2), near(q3), near(k_all), near(pos),
    )
    parts = lax.all_to_all(parts, ("yl", "core"), 0, 0, tiled=True)
    return call(place_kernel, (SUB, 8192), jnp.float32, near(parts), inside=False)


def solution(mesh):
    names = ("zh", "zl", "x", "yh", "yl", "core")
    fine = Mesh(mesh.devices.reshape(4, 4, 4, 2, 2, 2), names)
    ctx, head = names[:4], names[4:]
    in_specs = (P(ctx, head), P(ctx, None), P(), P(), P(ctx, head), P(ctx))
    return jax.shard_map(program, mesh=fine, in_specs=in_specs, out_specs=P(names, None), check_vma=False)
```

profile of v0, /device:TPU:352, one launch (start us, length us, event | category | flops | bytes accessed | tf_op | source)
XLA Modules:
  0.0 48.8 jit_solution(8435229775228767739)
XLA Ops:
  0.0 0.1 shard_map.73
  0.1 0.1 shard_map.74
  0.2 1.5 %shard_map.75 = (bf16[144,1024]{1,0:T(8,128)(2,1)S(1)}, bf16[64,128]{1,0:T(8,128)(2,1)S(1)}) custom-call(bf16[64,128]{1,0:T(8,128)(2,1)} %refs_0_.5, f32[1,128]{1,0:T(1,128)} %bitcast.13, f32[1,128]{1,0:T(1,128)} %bitcast.16, s32[1,64]{1,0:T(1,128)} %bitcast.6, f32[32,1]{1,0:T(8,128)} %constant.2.clone.refs_4_, ...), custom_call_target="tpu_custom_call", output_to_operand_aliasing={{0}: (8, {})} | custom-call | tf_op jit(solution)/shard_map/pallas_call | solution.py:124
  1.7 3.5 %collective-permute-start = (bf16[144,1024]{1,0:T(8,128)(2,1)S(1)}, bf16[144,1024]{1,0:T(8,128)(2,1)S(1)}, u32[]{:S(2)}, u32[]{:S(2)}) collective-permute-start(bf16[144,1024]{1,0:T(8,128)(2,1)S(1)} %get-tuple-element.15.q0), channel_id=1, source_target_pairs={{0,2},{2,0},{1,3},{3,1},{4,6},{6,4},{5,7},{7,5},{8,10},{10,8},{9,1... | collective-permute-start | bytes 884744 | tf_op jit(solution)/shard_map/ppermute | solution.py:252
  5.2 0.7 %collective-permute-start.3 = (bf16[64,128]{1,0:T(8,128)(2,1)S(1)}, bf16[64,128]{1,0:T(8,128)(2,1)S(1)}, u32[]{:S(2)}, u32[]{:S(2)}) collective-permute-start(bf16[64,128]{1,0:T(8,128)(2,1)S(1)} %get-tuple-element.11.refs_7_), channel_id=1, source_target_pairs={{0,0},{1,33},{2,66},{3,99},{4,68},{5,101},{6,6},{7,39},{32,32},{33... | collective-permute-start | bytes 49160 | tf_op jit(solution)/shard_map/ppermute | solution.py:245
  5.9 0.7 %collective-permute-start.4 = (bf16[64,128]{1,0:T(8,128)(2,1)S(1)}, bf16[64,128]{1,0:T(8,128)(2,1)S(1)}, u32[]{:S(2)}, u32[]{:S(2)}) collective-permute-start(bf16[64,128]{1,0:T(8,128)(2,1)S(1)} %get-tuple-element.13.refs_7_), channel_id=1, source_target_pairs={{128,128},{129,161},{130,194},{131,227},{132,196},{133,229},{134,1... | collective-permute-start | bytes 49160 | tf_op jit(solution)/shard_map/ppermute | solution.py:248
  6.5 0.0 collective-permute-done.3.own_0
  6.6 0.7 %collective-permute-start.6 = (bf16[64,128]{1,0:T(8,128)(2,1)S(1)}, bf16[64,128]{1,0:T(8,128)(2,1)S(1)}, u32[]{:S(2)}, u32[]{:S(2)}) collective-permute-start(bf16[64,128]{1,0:T(8,128)(2,1)S(1)} %collective-permute-done.3.own_0), channel_id=1, source_target_pairs={{0,128},{1,129},{2,130},{3,131},{4,132},{5,133},{6,134},{7,135},{3... | collective-permute-start | bytes 49160 | tf_op jit(solution)/shard_map/ppermute | solution.py:246
  7.2 0.7 %collective-permute-start.5 = (bf16[64,128]{1,0:T(8,128)(2,1)S(1)}, bf16[64,128]{1,0:T(8,128)(2,1)S(1)}, u32[]{:S(2)}, u32[]{:S(2)}) collective-permute-start(bf16[64,128]{1,0:T(8,128)(2,1)S(1)} %get-tuple-element.16), channel_id=1, source_target_pairs={{256,256},{257,289},{258,322},{259,355},{260,324},{261,357},{262,2... | collective-permute-start | bytes 49160 | tf_op jit(solution)/shard_map/ppermute | solution.py:254
  7.9 0.0 collective-permute-done.4.own_13
  7.9 1.3 %collective-permute-start.7 = (bf16[64,128]{1,0:T(8,128)(2,1)S(1)}, bf16[64,128]{1,0:T(8,128)(2,1)S(1)}, u32[]{:S(2)}, u32[]{:S(2)}) collective-permute-start(bf16[64,128]{1,0:T(8,128)(2,1)S(1)} %collective-permute-done.4.own_13), channel_id=1, source_target_pairs={{128,256},{129,257},{130,258},{131,259},{132,260},{133,261},{134,2... | collective-permute-start | bytes 49160 | tf_op jit(solution)/shard_map/ppermute | solution.py:253
  9.2 0.0 collective-permute-done.6.from_0
  9.2 1.3 %collective-permute-start.8 = (bf16[64,128]{1,0:T(8,128)(2,1)S(1)}, bf16[64,128]{1,0:T(8,128)(2,1)S(1)}, u32[]{:S(2)}, u32[]{:S(2)}) collective-permute-start(bf16[64,128]{1,0:T(8,128)(2,1)S(1)} %collective-permute-done.6.from_0), channel_id=1, source_target_pairs={{128,256},{129,257},{130,258},{131,259},{132,260},{133,261},{134,2... | collective-permute-start | bytes 49160 | tf_op jit(solution)/shard_map/ppermute | solution.py:249
  10.5 0.0 collective-permute-done.5.own_2
  10.5 6.9 %collective-permute-done.7.near_by = bf16[64,128]{1,0:T(8,128)(2,1)S(1)} collective-permute-done((bf16[64,128]{1,0:T(8,128)(2,1)S(1)}, bf16[64,128]{1,0:T(8,128)(2,1)S(1)}, u32[]{:S(2)}, u32[]{:S(2)}) %collective-permute-start.7) | collective-permute-done | bytes 16416 | tf_op jit(solution)/shard_map/ppermute | solution.py:253
  17.4 3.5 %collective-permute-done.8.far_off = bf16[64,128]{1,0:T(8,128)(2,1)S(1)} collective-permute-done((bf16[64,128]{1,0:T(8,128)(2,1)S(1)}, bf16[64,128]{1,0:T(8,128)(2,1)S(1)}, u32[]{:S(2)}, u32[]{:S(2)}) %collective-permute-start.8) | collective-permute-done | bytes 16416 | tf_op jit(solution)/shard_map/ppermute | solution.py:249
  20.9 0.8 %shard_map.76 = bf16[8,3,64,128]{3,2,1,0:T(8,128)(2,1)} custom-call(bf16[64,128]{1,0:T(8,128)(2,1)S(1)} %collective-permute-done.3.own_0, bf16[64,128]{1,0:T(8,128)(2,1)S(1)} %collective-permute-done.4.own_13, bf16[64,128]{1,0:T(8,128)(2,1)S(1)} %collective-permute-done.5.own_2, bf16[64,128]{1,0:T(8,128)(2,1)S(1)} %collective-permute-done.6.from_0, ...), custom_call_target="tpu_custom_call" | custom-call | tf_op jit(solution)/shard_map/pallas_call | solution.py:213
  21.7 0.0 copy-start
  21.7 6.0 %all-to-all-start = ((bf16[8,3,64,128]{3,2,1,0:T(8,128)(2,1)}), bf16[8,3,64,128]{3,2,1,0:T(8,128)(2,1)S(1)}, u32[]{:S(2)}, u32[]{:S(2)}) async-start(bf16[8,3,64,128]{3,2,1,0:T(8,128)(2,1)} %shard_map.76), calls=%async_computation | async-start | bytes 786432 | tf_op jit(solution)/shard_map/all_to_all | solution.py:262
  27.8 1.9 %collective-permute-start.1 = (bf16[144,1024]{1,0:T(8,128)(2,1)S(1)}, bf16[144,1024]{1,0:T(8,128)(2,1)S(1)}, u32[]{:S(2)}, u32[]{:S(2)}) collective-permute-start(bf16[144,1024]{1,0:T(8,128)(2,1)S(1)} %get-tuple-element.15.q0), channel_id=1, source_target_pairs={{0,1},{1,0},{2,3},{3,2},{4,5},{5,4},{6,7},{7,6},{8,9},{9,8},{10,11... | collective-permute-start | bytes 884744 | tf_op jit(solution)/shard_map/ppermute | solution.py:255
  29.7 0.0 collective-permute-done.q1
  29.7 2.4 %collective-permute-start.2 = (bf16[144,1024]{1,0:T(8,128)(2,1)S(1)}, bf16[144,1024]{1,0:T(8,128)(2,1)S(1)}, u32[]{:S(2)}, u32[]{:S(2)}) collective-permute-start(bf16[144,1024]{1,0:T(8,128)(2,1)S(1)} %collective-permute-done.q1), channel_id=1, source_target_pairs={{0,1},{1,0},{2,3},{3,2},{4,5},{5,4},{6,7},{7,6},{8,9},{9,8},{10,11... | collective-permute-start | bytes 884744 | tf_op jit(solution)/shard_map/ppermute | solution.py:256
  32.1 0.0 collective-permute-done.1.q2
  32.1 4.3 %all-to-all-done.k = bf16[8,3,64,128]{3,2,1,0:T(8,128)(2,1)S(1)} async-done(((bf16[8,3,64,128]{3,2,1,0:T(8,128)(2,1)}), bf16[8,3,64,128]{3,2,1,0:T(8,128)(2,1)S(1)}, u32[]{:S(2)}, u32[]{:S(2)}) %all-to-all-start) | async-done | bytes 393248 | tf_op jit(solution)/shard_map/all_to_all | solution.py:262
  36.5 0.0 collective-permute-done.2.q3
  36.5 0.0 copy-done
  36.5 3.3 %shard_map.77 = bf16[4,3,16,512]{3,2,1,0:T(8,128)(2,1)S(1)} custom-call(bf16[144,1024]{1,0:T(8,128)(2,1)S(1)} %get-tuple-element.15.q0, bf16[144,1024]{1,0:T(8,128)(2,1)S(1)} %collective-permute-done.q1, bf16[144,1024]{1,0:T(8,128)(2,1)S(1)} %collective-permute-done.1.q2, bf16[144,1024]{1,0:T(8,128)(2,1)S(1)} %collective-permute-done.2.q3, ...), custom_call_target="tpu_custom_call" | custom-call | tf_op jit(solution)/shard_map/pallas_call | solution.py:213
  39.7 8.2 %all_to_all.10.parts = bf16[4,3,16,512]{3,2,1,0:T(8,128)(2,1)S(1)} all-to-all(bf16[4,3,16,512]{3,2,1,0:T(8,128)(2,1)S(1)} %shard_map.77), channel_id=1, replica_groups=mesh['zh'=4,'zl'=4,'x'=4,'yh'=2,'yl'=2,'core'=2] {'yl','core'}, dimensions={0} | all-to-all | bytes 393216 | tf_op jit(solution)/shard_map/all_to_all | solution.py:270
  47.9 0.9 %shard_map.78 = f32[16,8192]{1,0:T(8,128)} custom-call(bf16[4,3,16,512]{3,2,1,0:T(8,128)(2,1)S(1)} %all_to_all.10.parts), custom_call_target="tpu_custom_call" | custom-call | tf_op jit(solution)/shard_map/pallas_call | solution.py:213
Async XLA Ops:
  1.7 28.0 %collective-permute-start = (bf16[144,1024]{1,0:T(8,128)(2,1)S(1)}, bf16[144,1024]{1,0:T(8,128)(2,1)S(1)}, u32[]{:S(2)}, u32[]{:S(2)}) collective-permute-start(bf16[144,1024]{1,0:T(8,128)(2,1)S(1)} %get-tuple-element.15.q0), channel_id=1, source_target_pairs={{0,2},{2,0},{1,3},{3,1},{4,6},{6,4},{5,7},{7,5},{8,10},{10,8},{9,1... | collective-permute-start | bytes 884744 | tf_op jit(solution)/shard_map/ppermute | solution.py:252
  5.2 1.3 %collective-permute-start.3 = (bf16[64,128]{1,0:T(8,128)(2,1)S(1)}, bf16[64,128]{1,0:T(8,128)(2,1)S(1)}, u32[]{:S(2)}, u32[]{:S(2)}) collective-permute-start(bf16[64,128]{1,0:T(8,128)(2,1)S(1)} %get-tuple-element.11.refs_7_), channel_id=1, source_target_pairs={{0,0},{1,33},{2,66},{3,99},{4,68},{5,101},{6,6},{7,39},{32,32},{33... | collective-permute-start | bytes 49160 | tf_op jit(solution)/shard_map/ppermute | solution.py:245
  5.9 2.0 %collective-permute-start.4 = (bf16[64,128]{1,0:T(8,128)(2,1)S(1)}, bf16[64,128]{1,0:T(8,128)(2,1)S(1)}, u32[]{:S(2)}, u32[]{:S(2)}) collective-permute-start(bf16[64,128]{1,0:T(8,128)(2,1)S(1)} %get-tuple-element.13.refs_7_), channel_id=1, source_target_pairs={{128,128},{129,161},{130,194},{131,227},{132,196},{133,229},{134,1... | collective-permute-start | bytes 49160 | tf_op jit(solution)/shard_map/ppermute | solution.py:248
  6.6 2.7 %collective-permute-start.6 = (bf16[64,128]{1,0:T(8,128)(2,1)S(1)}, bf16[64,128]{1,0:T(8,128)(2,1)S(1)}, u32[]{:S(2)}, u32[]{:S(2)}) collective-permute-start(bf16[64,128]{1,0:T(8,128)(2,1)S(1)} %collective-permute-done.3.own_0), channel_id=1, source_target_pairs={{0,128},{1,129},{2,130},{3,131},{4,132},{5,133},{6,134},{7,135},{3... | collective-permute-start | bytes 49160 | tf_op jit(solution)/shard_map/ppermute | solution.py:246
  7.2 3.3 %collective-permute-start.5 = (bf16[64,128]{1,0:T(8,128)(2,1)S(1)}, bf16[64,128]{1,0:T(8,128)(2,1)S(1)}, u32[]{:S(2)}, u32[]{:S(2)}) collective-permute-start(bf16[64,128]{1,0:T(8,128)(2,1)S(1)} %get-tuple-element.16), channel_id=1, source_target_pairs={{256,256},{257,289},{258,322},{259,355},{260,324},{261,357},{262,2... | collective-permute-start | bytes 49160 | tf_op jit(solution)/shard_map/ppermute | solution.py:254
  7.9 9.5 %collective-permute-start.7 = (bf16[64,128]{1,0:T(8,128)(2,1)S(1)}, bf16[64,128]{1,0:T(8,128)(2,1)S(1)}, u32[]{:S(2)}, u32[]{:S(2)}) collective-permute-start(bf16[64,128]{1,0:T(8,128)(2,1)S(1)} %collective-permute-done.4.own_13), channel_id=1, source_target_pairs={{128,256},{129,257},{130,258},{131,259},{132,260},{133,261},{134,2... | collective-permute-start | bytes 49160 | tf_op jit(solution)/shard_map/ppermute | solution.py:253
  9.2 11.7 %collective-permute-start.8 = (bf16[64,128]{1,0:T(8,128)(2,1)S(1)}, bf16[64,128]{1,0:T(8,128)(2,1)S(1)}, u32[]{:S(2)}, u32[]{:S(2)}) collective-permute-start(bf16[64,128]{1,0:T(8,128)(2,1)S(1)} %collective-permute-done.6.from_0), channel_id=1, source_target_pairs={{128,256},{129,257},{130,258},{131,259},{132,260},{133,261},{134,2... | collective-permute-start | bytes 49160 | tf_op jit(solution)/shard_map/ppermute | solution.py:249
  21.7 14.7 %copy-start = (s32[64]{0:T(128)S(1)}, s32[64]{0:T(128)}, u32[]{:S(2)}) copy-start(s32[64]{0:T(128)} %param.12) | copy-start | bytes 772
  21.7 14.7 %all-to-all-start = ((bf16[8,3,64,128]{3,2,1,0:T(8,128)(2,1)}), bf16[8,3,64,128]{3,2,1,0:T(8,128)(2,1)S(1)}, u32[]{:S(2)}, u32[]{:S(2)}) async-start(bf16[8,3,64,128]{3,2,1,0:T(8,128)(2,1)} %shard_map.76), calls=%async_computation | async-start | bytes 786432 | tf_op jit(solution)/shard_map/all_to_all | solution.py:262
  27.8 4.3 %collective-permute-start.1 = (bf16[144,1024]{1,0:T(8,128)(2,1)S(1)}, bf16[144,1024]{1,0:T(8,128)(2,1)S(1)}, u32[]{:S(2)}, u32[]{:S(2)}) collective-permute-start(bf16[144,1024]{1,0:T(8,128)(2,1)S(1)} %get-tuple-element.15.q0), channel_id=1, source_target_pairs={{0,1},{1,0},{2,3},{3,2},{4,5},{5,4},{6,7},{7,6},{8,9},{9,8},{10,11... | collective-permute-start | bytes 884744 | tf_op jit(solution)/shard_map/ppermute | solution.py:255
  29.7 6.7 %collective-permute-start.2 = (bf16[144,1024]{1,0:T(8,128)(2,1)S(1)}, bf16[144,1024]{1,0:T(8,128)(2,1)S(1)}, u32[]{:S(2)}, u32[]{:S(2)}) collective-permute-start(bf16[144,1024]{1,0:T(8,128)(2,1)S(1)} %collective-permute-done.q1), channel_id=1, source_target_pairs={{0,1},{1,0},{2,3},{3,2},{4,5},{5,4},{6,7},{7,6},{8,9},{9,8},{10,11... | collective-permute-start | bytes 884744 | tf_op jit(solution)/shard_map/ppermute | solution.py:256
where the time goes:
time: 49.2 us; the launch traced here: 48.8 us
  starting transfers between devices  19.1 us (39%)
  waiting for transfers between devices  14.7 us (30%)
  blocking collectives  8.21 us (17%)
  Pallas kernels  6.61 us (13%)
    all_to_all x1, blocking collectives, program(): parts = lax.all_to_all(parts, ('yl', 'core'), 0, 0, tiled=True)  8.21 us
    ppermute x1, waiting for transfers between devices, program(): near_by = lax.ppermute(own_13, LINE, hop(1, 2, False))  6.92 us
    all_to_all x1, starting transfers between devices, program(): lax.all_to_all(sent, ('x', 'yh', 'yl'), 0, 0, axis_index_groups=NEAR, til...  6.05 us
    pallas_call x3, Pallas kernels, call(): pl.pallas_call(kernel, out_shape=out, in_specs=[VMEM] * len(args), out_sp...  4.92 us
    all_to_all x1, waiting for transfers between devices, program(): lax.all_to_all(sent, ('x', 'yh', 'yl'), 0, 0, axis_index_groups=NEAR, til...  4.32 us
    ppermute x1, waiting for transfers between devices, program(): far_off = lax.ppermute(from_0, LINE, hop(1, 2, False))  3.49 us
    ppermute x1, starting transfers between devices, program(): q1 = lax.ppermute(q0, 'yl', swap)  3.48 us
    ppermute x1, starting transfers between devices, program(): q3 = lax.ppermute(q1, 'core', swap)  2.41 us
  transfers between devices with their start and end apart: 10, of which 3 were waited for; matrix products, arithmetic and copies ran while one was open for 0% of the time, Pallas kernels for 2%

commit v1 on v0

--- a/solution.py
+++ b/solution.py
@@ -151,9 +151,9 @@
         acc = jnp.zeros((n, DH), jnp.float32)
         for q in (q0, q1, q2, q3):
             w = q[DH : DH + 1, :].astype(jnp.float32)
-            for c in range(0, QT, 512):
-                s = jnp.dot(kk, q[:DH, c : c + 512], preferred_element_type=jnp.float32)
-                for p in range(0, 512, DH):
+            for c in range(0, QT, 1024):
+                s = jnp.dot(kk, q[:DH, c : c + 1024], preferred_element_type=jnp.float32)
+                for p in range(0, 1024, DH):
                     acc = acc + jnp.maximum(s[:, p : p + DH], 0.0) * w[:, c + p : c + p + DH]
         acc = acc.T
         acc = acc[:ROWS] + acc[ROWS:]

time: 49.2 us -> 49.2 us (level)
  no operation moved by 1% of the time
where the time goes in v1:
time: 49.2 us; the launch traced here: 48.8 us
  starting transfers between devices  19.1 us (39%)
  waiting for transfers between devices  14.7 us (30%)
  blocking collectives  8.21 us (17%)
  Pallas kernels  6.61 us (13%)
    all_to_all x1, blocking collectives, program(): parts = lax.all_to_all(parts, ('yl', 'core'), 0, 0, tiled=True)  8.21 us
    ppermute x1, waiting for transfers between devices, program(): near_by = lax.ppermute(own_13, LINE, hop(1, 2, False))  6.92 us
    all_to_all x1, starting transfers between devices, program(): lax.all_to_all(sent, ('x', 'yh', 'yl'), 0, 0, axis_index_groups=NEAR, til...  6.05 us
    pallas_call x3, Pallas kernels, call(): pl.pallas_call(kernel, out_shape=out, in_specs=[VMEM] * len(args), out_sp...  4.92 us
    all_to_all x1, waiting for transfers between devices, program(): lax.all_to_all(sent, ('x', 'yh', 'yl'), 0, 0, axis_index_groups=NEAR, til...  4.32 us
    ppermute x1, waiting for transfers between devices, program(): far_off = lax.ppermute(from_0, LINE, hop(1, 2, False))  3.49 us
    ppermute x1, starting transfers between devices, program(): q1 = lax.ppermute(q0, 'yl', swap)  3.48 us
    ppermute x1, starting transfers between devices, program(): q3 = lax.ppermute(q1, 'core', swap)  2.41 us
  transfers between devices with their start and end apart: 10, of which 3 were waited for; matrix products, arithmetic and copies ran while one was open for 0% of the time, Pallas kernels for 2%

profile of v1, /device:TPU:352, one launch (start us, length us, event | category | flops | bytes accessed | tf_op | source)
XLA Modules:
  0.0 48.8 jit_solution(8435229775228767739)
XLA Ops:
  0.0 0.1 shard_map.73
  0.1 0.1 shard_map.74
  0.2 1.5 %shard_map.75 = (bf16[144,1024]{1,0:T(8,128)(2,1)S(1)}, bf16[64,128]{1,0:T(8,128)(2,1)S(1)}) custom-call(bf16[64,128]{1,0:T(8,128)(2,1)} %refs_0_.5, f32[1,128]{1,0:T(1,128)} %bitcast.13, f32[1,128]{1,0:T(1,128)} %bitcast.16, s32[1,64]{1,0:T(1,128)} %bitcast.6, f32[32,1]{1,0:T(8,128)} %constant.2.clone.refs_4_, ...), custom_call_target="tpu_custom_call", output_to_operand_aliasing={{0}: (8, {})} | custom-call | tf_op jit(solution)/shard_map/pallas_call | solution.py:124
  1.7 3.5 %collective-permute-start = (bf16[144,1024]{1,0:T(8,128)(2,1)S(1)}, bf16[144,1024]{1,0:T(8,128)(2,1)S(1)}, u32[]{:S(2)}, u32[]{:S(2)}) collective-permute-start(bf16[144,1024]{1,0:T(8,128)(2,1)S(1)} %get-tuple-element.15.q0), channel_id=1, source_target_pairs={{0,2},{2,0},{1,3},{3,1},{4,6},{6,4},{5,7},{7,5},{8,10},{10,8},{9,1... | collective-permute-start | bytes 884744 | tf_op jit(solution)/shard_map/ppermute | solution.py:252
  5.2 0.7 %collective-permute-start.3 = (bf16[64,128]{1,0:T(8,128)(2,1)S(1)}, bf16[64,128]{1,0:T(8,128)(2,1)S(1)}, u32[]{:S(2)}, u32[]{:S(2)}) collective-permute-start(bf16[64,128]{1,0:T(8,128)(2,1)S(1)} %get-tuple-element.11.refs_7_), channel_id=1, source_target_pairs={{0,0},{1,33},{2,66},{3,99},{4,68},{5,101},{6,6},{7,39},{32,32},{33... | collective-permute-start | bytes 49160 | tf_op jit(solution)/shard_map/ppermute | solution.py:245
  5.9 0.7 %collective-permute-start.4 = (bf16[64,128]{1,0:T(8,128)(2,1)S(1)}, bf16[64,128]{1,0:T(8,128)(2,1)S(1)}, u32[]{:S(2)}, u32[]{:S(2)}) collective-permute-start(bf16[64,128]{1,0:T(8,128)(2,1)S(1)} %get-tuple-element.13.refs_7_), channel_id=1, source_target_pairs={{128,128},{129,161},{130,194},{131,227},{132,196},{133,229},{134,1... | collective-permute-start | bytes 49160 | tf_op jit(solution)/shard_map/ppermute | solution.py:248
  6.5 0.0 collective-permute-done.3.own_0
  6.6 0.7 %collective-permute-start.6 = (bf16[64,128]{1,0:T(8,128)(2,1)S(1)}, bf16[64,128]{1,0:T(8,128)(2,1)S(1)}, u32[]{:S(2)}, u32[]{:S(2)}) collective-permute-start(bf16[64,128]{1,0:T(8,128)(2,1)S(1)} %collective-permute-done.3.own_0), channel_id=1, source_target_pairs={{0,128},{1,129},{2,130},{3,131},{4,132},{5,133},{6,134},{7,135},{3... | collective-permute-start | bytes 49160 | tf_op jit(solution)/shard_map/ppermute | solution.py:246
  7.2 0.7 %collective-permute-start.5 = (bf16[64,128]{1,0:T(8,128)(2,1)S(1)}, bf16[64,128]{1,0:T(8,128)(2,1)S(1)}, u32[]{:S(2)}, u32[]{:S(2)}) collective-permute-start(bf16[64,128]{1,0:T(8,128)(2,1)S(1)} %get-tuple-element.16), channel_id=1, source_target_pairs={{256,256},{257,289},{258,322},{259,355},{260,324},{261,357},{262,2... | collective-permute-start | bytes 49160 | tf_op jit(solution)/shard_map/ppermute | solution.py:254
  7.9 0.0 collective-permute-done.4.own_13
  7.9 1.3 %collective-permute-start.7 = (bf16[64,128]{1,0:T(8,128)(2,1)S(1)}, bf16[64,128]{1,0:T(8,128)(2,1)S(1)}, u32[]{:S(2)}, u32[]{:S(2)}) collective-permute-start(bf16[64,128]{1,0:T(8,128)(2,1)S(1)} %collective-permute-done.4.own_13), channel_id=1, source_target_pairs={{128,256},{129,257},{130,258},{131,259},{132,260},{133,261},{134,2... | collective-permute-start | bytes 49160 | tf_op jit(solution)/shard_map/ppermute | solution.py:253
  9.2 0.0 collective-permute-done.6.from_0
  9.2 1.3 %collective-permute-start.8 = (bf16[64,128]{1,0:T(8,128)(2,1)S(1)}, bf16[64,128]{1,0:T(8,128)(2,1)S(1)}, u32[]{:S(2)}, u32[]{:S(2)}) collective-permute-start(bf16[64,128]{1,0:T(8,128)(2,1)S(1)} %collective-permute-done.6.from_0), channel_id=1, source_target_pairs={{128,256},{129,257},{130,258},{131,259},{132,260},{133,261},{134,2... | collective-permute-start | bytes 49160 | tf_op jit(solution)/shard_map/ppermute | solution.py:249
  10.5 0.0 collective-permute-done.5.own_2
  10.5 6.9 %collective-permute-done.7.near_by = bf16[64,128]{1,0:T(8,128)(2,1)S(1)} collective-permute-done((bf16[64,128]{1,0:T(8,128)(2,1)S(1)}, bf16[64,128]{1,0:T(8,128)(2,1)S(1)}, u32[]{:S(2)}, u32[]{:S(2)}) %collective-permute-start.7) | collective-permute-done | bytes 16416 | tf_op jit(solution)/shard_map/ppermute | solution.py:253
  17.4 3.5 %collective-permute-done.8.far_off = bf16[64,128]{1,0:T(8,128)(2,1)S(1)} collective-permute-done((bf16[64,128]{1,0:T(8,128)(2,1)S(1)}, bf16[64,128]{1,0:T(8,128)(2,1)S(1)}, u32[]{:S(2)}, u32[]{:S(2)}) %collective-permute-start.8) | collective-permute-done | bytes 16416 | tf_op jit(solution)/shard_map/ppermute | solution.py:249
  20.9 0.8 %shard_map.76 = bf16[8,3,64,128]{3,2,1,0:T(8,128)(2,1)} custom-call(bf16[64,128]{1,0:T(8,128)(2,1)S(1)} %collective-permute-done.3.own_0, bf16[64,128]{1,0:T(8,128)(2,1)S(1)} %collective-permute-done.4.own_13, bf16[64,128]{1,0:T(8,128)(2,1)S(1)} %collective-permute-done.5.own_2, bf16[64,128]{1,0:T(8,128)(2,1)S(1)} %collective-permute-done.6.from_0, ...), custom_call_target="tpu_custom_call" | custom-call | tf_op jit(solution)/shard_map/pallas_call | solution.py:213
  21.7 0.0 copy-start
  21.7 6.0 %all-to-all-start = ((bf16[8,3,64,128]{3,2,1,0:T(8,128)(2,1)}), bf16[8,3,64,128]{3,2,1,0:T(8,128)(2,1)S(1)}, u32[]{:S(2)}, u32[]{:S(2)}) async-start(bf16[8,3,64,128]{3,2,1,0:T(8,128)(2,1)} %shard_map.76), calls=%async_computation | async-start | bytes 786432 | tf_op jit(solution)/shard_map/all_to_all | solution.py:262
  27.8 1.9 %collective-permute-start.1 = (bf16[144,1024]{1,0:T(8,128)(2,1)S(1)}, bf16[144,1024]{1,0:T(8,128)(2,1)S(1)}, u32[]{:S(2)}, u32[]{:S(2)}) collective-permute-start(bf16[144,1024]{1,0:T(8,128)(2,1)S(1)} %get-tuple-element.15.q0), channel_id=1, source_target_pairs={{0,1},{1,0},{2,3},{3,2},{4,5},{5,4},{6,7},{7,6},{8,9},{9,8},{10,11... | collective-permute-start | bytes 884744 | tf_op jit(solution)/shard_map/ppermute | solution.py:255
  29.7 0.0 collective-permute-done.q1
  29.7 2.4 %collective-permute-start.2 = (bf16[144,1024]{1,0:T(8,128)(2,1)S(1)}, bf16[144,1024]{1,0:T(8,128)(2,1)S(1)}, u32[]{:S(2)}, u32[]{:S(2)}) collective-permute-start(bf16[144,1024]{1,0:T(8,128)(2,1)S(1)} %collective-permute-done.q1), channel_id=1, source_target_pairs={{0,1},{1,0},{2,3},{3,2},{4,5},{5,4},{6,7},{7,6},{8,9},{9,8},{10,11... | collective-permute-start | bytes 884744 | tf_op jit(solution)/shard_map/ppermute | solution.py:256
  32.1 0.0 collective-permute-done.1.q2
  32.1 4.3 %all-to-all-done.k = bf16[8,3,64,128]{3,2,1,0:T(8,128)(2,1)S(1)} async-done(((bf16[8,3,64,128]{3,2,1,0:T(8,128)(2,1)}), bf16[8,3,64,128]{3,2,1,0:T(8,128)(2,1)S(1)}, u32[]{:S(2)}, u32[]{:S(2)}) %all-to-all-start) | async-done | bytes 393248 | tf_op jit(solution)/shard_map/all_to_all | solution.py:262
  36.5 0.0 collective-permute-done.2.q3
  36.5 0.0 copy-done
  36.5 3.3 %shard_map.77 = bf16[4,3,16,512]{3,2,1,0:T(8,128)(2,1)S(1)} custom-call(bf16[144,1024]{1,0:T(8,128)(2,1)S(1)} %get-tuple-element.15.q0, bf16[144,1024]{1,0:T(8,128)(2,1)S(1)} %collective-permute-done.q1, bf16[144,1024]{1,0:T(8,128)(2,1)S(1)} %collective-permute-done.1.q2, bf16[144,1024]{1,0:T(8,128)(2,1)S(1)} %collective-permute-done.2.q3, ...), custom_call_target="tpu_custom_call" | custom-call | tf_op jit(solution)/shard_map/pallas_call | solution.py:213
  39.7 8.2 %all_to_all.10.parts = bf16[4,3,16,512]{3,2,1,0:T(8,128)(2,1)S(1)} all-to-all(bf16[4,3,16,512]{3,2,1,0:T(8,128)(2,1)S(1)} %shard_map.77), channel_id=1, replica_groups=mesh['zh'=4,'zl'=4,'x'=4,'yh'=2,'yl'=2,'core'=2] {'yl','core'}, dimensions={0} | all-to-all | bytes 393216 | tf_op jit(solution)/shard_map/all_to_all | solution.py:270
  47.9 0.9 %shard_map.78 = f32[16,8192]{1,0:T(8,128)} custom-call(bf16[4,3,16,512]{3,2,1,0:T(8,128)(2,1)S(1)} %all_to_all.10.parts), custom_call_target="tpu_custom_call" | custom-call | tf_op jit(solution)/shard_map/pallas_call | solution.py:213
Async XLA Ops:
  1.7 28.0 %collective-permute-start = (bf16[144,1024]{1,0:T(8,128)(2,1)S(1)}, bf16[144,1024]{1,0:T(8,128)(2,1)S(1)}, u32[]{:S(2)}, u32[]{:S(2)}) collective-permute-start(bf16[144,1024]{1,0:T(8,128)(2,1)S(1)} %get-tuple-element.15.q0), channel_id=1, source_target_pairs={{0,2},{2,0},{1,3},{3,1},{4,6},{6,4},{5,7},{7,5},{8,10},{10,8},{9,1... | collective-permute-start | bytes 884744 | tf_op jit(solution)/shard_map/ppermute | solution.py:252
  5.2 1.3 %collective-permute-start.3 = (bf16[64,128]{1,0:T(8,128)(2,1)S(1)}, bf16[64,128]{1,0:T(8,128)(2,1)S(1)}, u32[]{:S(2)}, u32[]{:S(2)}) collective-permute-start(bf16[64,128]{1,0:T(8,128)(2,1)S(1)} %get-tuple-element.11.refs_7_), channel_id=1, source_target_pairs={{0,0},{1,33},{2,66},{3,99},{4,68},{5,101},{6,6},{7,39},{32,32},{33... | collective-permute-start | bytes 49160 | tf_op jit(solution)/shard_map/ppermute | solution.py:245
  5.9 2.0 %collective-permute-start.4 = (bf16[64,128]{1,0:T(8,128)(2,1)S(1)}, bf16[64,128]{1,0:T(8,128)(2,1)S(1)}, u32[]{:S(2)}, u32[]{:S(2)}) collective-permute-start(bf16[64,128]{1,0:T(8,128)(2,1)S(1)} %get-tuple-element.13.refs_7_), channel_id=1, source_target_pairs={{128,128},{129,161},{130,194},{131,227},{132,196},{133,229},{134,1... | collective-permute-start | bytes 49160 | tf_op jit(solution)/shard_map/ppermute | solution.py:248
  6.6 2.7 %collective-permute-start.6 = (bf16[64,128]{1,0:T(8,128)(2,1)S(1)}, bf16[64,128]{1,0:T(8,128)(2,1)S(1)}, u32[]{:S(2)}, u32[]{:S(2)}) collective-permute-start(bf16[64,128]{1,0:T(8,128)(2,1)S(1)} %collective-permute-done.3.own_0), channel_id=1, source_target_pairs={{0,128},{1,129},{2,130},{3,131},{4,132},{5,133},{6,134},{7,135},{3... | collective-permute-start | bytes 49160 | tf_op jit(solution)/shard_map/ppermute | solution.py:246
  7.2 3.3 %collective-permute-start.5 = (bf16[64,128]{1,0:T(8,128)(2,1)S(1)}, bf16[64,128]{1,0:T(8,128)(2,1)S(1)}, u32[]{:S(2)}, u32[]{:S(2)}) collective-permute-start(bf16[64,128]{1,0:T(8,128)(2,1)S(1)} %get-tuple-element.16), channel_id=1, source_target_pairs={{256,256},{257,289},{258,322},{259,355},{260,324},{261,357},{262,2... | collective-permute-start | bytes 49160 | tf_op jit(solution)/shard_map/ppermute | solution.py:254
  7.9 9.5 %collective-permute-start.7 = (bf16[64,128]{1,0:T(8,128)(2,1)S(1)}, bf16[64,128]{1,0:T(8,128)(2,1)S(1)}, u32[]{:S(2)}, u32[]{:S(2)}) collective-permute-start(bf16[64,128]{1,0:T(8,128)(2,1)S(1)} %collective-permute-done.4.own_13), channel_id=1, source_target_pairs={{128,256},{129,257},{130,258},{131,259},{132,260},{133,261},{134,2... | collective-permute-start | bytes 49160 | tf_op jit(solution)/shard_map/ppermute | solution.py:253
  9.2 11.7 %collective-permute-start.8 = (bf16[64,128]{1,0:T(8,128)(2,1)S(1)}, bf16[64,128]{1,0:T(8,128)(2,1)S(1)}, u32[]{:S(2)}, u32[]{:S(2)}) collective-permute-start(bf16[64,128]{1,0:T(8,128)(2,1)S(1)} %collective-permute-done.6.from_0), channel_id=1, source_target_pairs={{128,256},{129,257},{130,258},{131,259},{132,260},{133,261},{134,2... | collective-permute-start | bytes 49160 | tf_op jit(solution)/shard_map/ppermute | solution.py:249
  21.7 14.7 %copy-start = (s32[64]{0:T(128)S(1)}, s32[64]{0:T(128)}, u32[]{:S(2)}) copy-start(s32[64]{0:T(128)} %param.12) | copy-start | bytes 772
  21.7 14.7 %all-to-all-start = ((bf16[8,3,64,128]{3,2,1,0:T(8,128)(2,1)}), bf16[8,3,64,128]{3,2,1,0:T(8,128)(2,1)S(1)}, u32[]{:S(2)}, u32[]{:S(2)}) async-start(bf16[8,3,64,128]{3,2,1,0:T(8,128)(2,1)} %shard_map.76), calls=%async_computation | async-start | bytes 786432 | tf_op jit(solution)/shard_map/all_to_all | solution.py:262
  27.8 4.3 %collective-permute-start.1 = (bf16[144,1024]{1,0:T(8,128)(2,1)S(1)}, bf16[144,1024]{1,0:T(8,128)(2,1)S(1)}, u32[]{:S(2)}, u32[]{:S(2)}) collective-permute-start(bf16[144,1024]{1,0:T(8,128)(2,1)S(1)} %get-tuple-element.15.q0), channel_id=1, source_target_pairs={{0,1},{1,0},{2,3},{3,2},{4,5},{5,4},{6,7},{7,6},{8,9},{9,8},{10,11... | collective-permute-start | bytes 884744 | tf_op jit(solution)/shard_map/ppermute | solution.py:255
  29.7 6.7 %collective-permute-start.2 = (bf16[144,1024]{1,0:T(8,128)(2,1)S(1)}, bf16[144,1024]{1,0:T(8,128)(2,1)S(1)}, u32[]{:S(2)}, u32[]{:S(2)}) collective-permute-start(bf16[144,1024]{1,0:T(8,128)(2,1)S(1)} %collective-permute-done.q1), channel_id=1, source_target_pairs={{0,1},{1,0},{2,3},{3,2},{4,5},{5,4},{6,7},{7,6},{8,9},{9,8},{10,11... | collective-permute-start | bytes 884744 | tf_op jit(solution)/shard_map/ppermute | solution.py:256
